TPU v7x, 32 devices: a whole 2x2x4 slice. The times are simulated.
32 devices in a mesh: row: 8 (over y, x, core), grp: 4 (over z).
Axes of the slice: x: 2, y: 2, z: 4, core: 2. Of those that a mesh axis runs over, the one named last changes fastest.
Arguments:
- positions: float32 [3, 1024], replicated, may hold values from -0.05 to 9.35, as said below
- detuning: float32 [1024], replicated, may hold values from -1 to 1
- populations: float32 [1024], P('row'), may hold values from 0 to 1
- base: float32 [2, 64, 1024], P(None, 'grp', 'row'), may hold values from -6 to 6
- section: float32 [2, 64, 1024], P(None, 'grp', 'row'), may hold values from -6 to 6
- accum: float32 [2, 64, 1024], P(None, 'grp', 'row'), may hold values from -3 to 3
Outputs:
- next_input: float32 [2, 64, 1024], P(None, 'grp', 'row')
- accum_out: float32 [2, 64, 1024], P(None, 'grp', 'row')
Inputs may be any that keep to these rules, and one draw needn't show every extreme that they name: `positions`: emitter n sits near the lattice point 0.3 * (n % 32, (n // 32) % 32, n // 1024), displaced by at most 0.05 in each coordinate.
All inputs are finite; a program needn't handle non-finite values.
Results may differ from a plain program's by a relative error of at most 0.0003.
Values sent between devices are 32-bit elements; how exact they have to be, the bound alone decides.
A program may use at most 64 MiB of HBM per device.

v0:
```python
import math
import jax
import jax.numpy as jnp
from jax import lax
from jax.sharding import PartitionSpec as P

WAVE_NUMBER = 2.0 * math.pi
TIME_STEP = 0.2


def coupling(pos_rows, pos_cols, row_ids, col_ids):
    offsets = pos_rows[:, :, None] - pos_cols[:, None, :]
    dist_sq = jnp.sum(offsets * offsets, axis=0)
    on_diag = row_ids[:, None] == col_ids[None, :]
    safe_sq = jnp.where(on_diag, 1.0, dist_sq)
    phase = WAVE_NUMBER * jnp.sqrt(safe_sq)
    inverse = 1.0 / phase
    inverse_sq = inverse * inverse
    aligned = offsets[2] * offsets[2] / safe_sq
    quad_real = 1.0 - inverse_sq - aligned * (1.0 - 3.0 * inverse_sq)
    quad_imag = inverse - 3.0 * aligned * inverse
    cosine = jnp.cos(phase)
    sine = jnp.sin(phase)
    h_real = -0.75 * inverse * (cosine * quad_real - sine * quad_imag)
    h_imag = -0.75 * inverse * (sine * quad_real + cosine * quad_imag)
    return (jnp.where(on_diag, 0.0, h_real), jnp.where(on_diag, 0.0, h_imag))


def cross_rows(slab_part, tile):
    return lax.dot_general(
        slab_part,
        tile,
        (((1,), (1,)), ((), ())),
        precision=lax.Precision.HIGHEST,
        preferred_element_type=jnp.float32,
    )


def lead_rows(tile, slab_part):
    return lax.dot_general(
        tile,
        slab_part,
        (((0,), (0,)), ((), ())),
        precision=lax.Precision.HIGHEST,
        preferred_element_type=jnp.float32,
    )


def slab_rate(
    z_real,
    z_imag,
    shift,
    local_slab,
    full_slab,
    local_det,
    slab_pos,
    slab_det,
    col_start,
    col_count,
):
    slab_ids = lax.iota(jnp.int32, slab_pos.shape[1])
    w_real, w_imag = coupling(slab_pos, slab_pos, slab_ids, slab_ids)
    eye_mask = slab_ids[:, None] == slab_ids[None, :]
    w_real = w_real + jnp.where(eye_mask, slab_det[:, None], 0.0)
    w_imag = w_imag + jnp.where(eye_mask, -0.5, 0.0)
    w_real = lax.dynamic_slice_in_dim(w_real, col_start, col_count, 1)
    w_imag = lax.dynamic_slice_in_dim(w_imag, col_start, col_count, 1)
    v_real = lead_rows(w_real, full_slab[0]) + lead_rows(w_imag, full_slab[1])
    v_imag = lead_rows(w_real, full_slab[1]) - lead_rows(w_imag, full_slab[0])
    y_real = local_slab[0]
    y_imag = local_slab[1]
    z_real = z_real + local_det * y_real + 0.5 * y_imag
    z_imag = z_imag + local_det * y_imag - 0.5 * y_real
    f_real = z_imag + shift * y_imag - v_imag
    f_imag = -z_real - shift * y_real + v_real
    return jnp.stack([f_real, f_imag])


def accumulate(totals, pieces, pos_rows, row_ids, positions):
    slab_piece, pop_piece = pieces
    piece_len = slab_piece.shape[2]
    block_len = math.gcd(piece_len, 512)
    signed_pops = 2.0 * pop_piece.reshape(piece_len) - 1.0

    def one_block(step_index, sums):
        offset = step_index * block_len
        slab_block = lax.dynamic_slice_in_dim(slab_piece, offset, block_len, 2)
        pop_block = lax.dynamic_slice_in_dim(signed_pops, offset, block_len, 0)
        pos_block = lax.dynamic_slice_in_dim(positions, offset, block_len, 1)
        col_ids = offset + lax.iota(jnp.int32, block_len)
        h_real, h_imag = coupling(pos_rows, pos_block, row_ids, col_ids)
        z_real = sums[0] + cross_rows(slab_block[0], h_real) - cross_rows(slab_block[1], h_imag)
        z_imag = sums[1] + cross_rows(slab_block[0], h_imag) + cross_rows(slab_block[1], h_real)
        shift = sums[2] + jnp.dot(h_real, pop_block, precision=lax.Precision.HIGHEST)
        return (z_real, z_imag, shift)

    return lax.fori_loop(0, piece_len // block_len, one_block, totals)


def local(positions, detuning, populations, base, section, accum):
    col_count = section.shape[1]
    slab_width = col_count * lax.axis_size("grp")
    row_count = section.shape[2]
    slab_pos = positions[:, :slab_width]
    slab_det = detuning[:slab_width]
    row_start = lax.axis_index("row") * row_count
    pos_rows = lax.dynamic_slice_in_dim(positions, row_start, row_count, 1)
    local_det = lax.dynamic_slice_in_dim(detuning, row_start, row_count, 0)
    row_ids = row_start + lax.iota(jnp.int32, row_count)
    full_slab = lax.all_gather(section, "grp", axis=1, tiled=True)
    pop_piece = populations.reshape(1, 1, row_count)
    zeros_cols = jnp.zeros((col_count, row_count), jnp.float32)
    initial = (zeros_cols, zeros_cols, jnp.zeros((row_count,), jnp.float32))
    z_real, z_imag, shift = accumulate(
        initial,
        (
            lax.all_gather(section, "row", axis=2, tiled=True),
            lax.all_gather(pop_piece, "row", axis=2, tiled=True),
        ),
        pos_rows,
        row_ids,
        positions,
    )
    col_start = lax.axis_index("grp") * col_count
    rate = slab_rate(
        z_real,
        z_imag,
        shift,
        section,
        full_slab,
        local_det,
        slab_pos,
        slab_det,
        col_start,
        col_count,
    )
    next_input = base + 0.5 * TIME_STEP * rate
    accum_out = accum + TIME_STEP / 3.0 * rate
    return (next_input, accum_out)


def solution(mesh):
    return jax.shard_map(
        local,
        mesh=mesh,
        in_specs=(
            P(),
            P(),
            P("row"),
            P(None, "grp", "row"),
            P(None, "grp", "row"),
            P(None, "grp", "row"),
        ),
        out_specs=(P(None, "grp", "row"), P(None, "grp", "row")),
        check_vma=False,
    )
```

profile of v0, /device:TPU:0, one launch (start us, length us, event | category | flops | bytes accessed | tf_op | source)
XLA Modules:
  0.0 47.5 jit_solution(1856652842638416693)
XLA Ops:
  0.6 0.0 copy-start.1
  0.6 0.0 copy-start.5
  0.7 0.7 %copy-done.5 = f32[1024]{0:T(1024)S(1)} copy-done((f32[1024]{0:T(1024)S(1)}, f32[1024]{0:T(1024)}, u32[]{:S(2)}) %copy-start.5) | copy-done | bytes 4120
  1.3 0.1 dynamic_slice.34
  1.4 0.0 copy-done.1
  1.4 0.0 copy-start.6
  1.4 0.0 copy-start
  1.4 0.6 %copy-done.6 = f32[128]{0:T(128)S(1)} copy-done((f32[128]{0:T(128)S(1)}, f32[128]{0:T(128)}, u32[]{:S(2)}) %copy-start.6) | copy-done | bytes 536
  2.1 10.3 %all-gather.1 = f32[8,1,128]{2,1,0:T(1,128)S(1)} all-gather(f32[1,1,128]{2,1,0:T(1,128)S(1)} %bitcast.145), channel_id=2, replica_groups=mesh['row'=8,'grp'=4] {'row'}, dimensions={0}, use_global_device_ids=true | all-gather | bytes 4608 | tf_op jit(solution)/shard_map/all_gather | solution.py:118
  12.4 0.0 copy-done
  12.4 0.0 slice-start
  12.4 13.4 %all_gather.11 = f32[2,64,128]{2,1,0:T(8,128)S(1)} all-gather(f32[2,16,128]{2,1,0:T(8,128)S(1)} %copy-done), channel_id=1, replica_groups=mesh['row'=8,'grp'=4] {'grp'}, dimensions={1}, use_global_device_ids=true | all-gather | bytes 81920 | tf_op jit(solution)/shard_map/all_gather | solution.py:110
  25.7 0.0 slice-done
  25.8 0.1 broadcast_subtract_fusion.1
  25.9 0.2 fusion.52
  26.0 0.0 slice-start.1
  26.0 0.6 %slice-done.1 = f32[64]{0:T(128)S(1)} async-done(((f32[1024]{0:T(1024)}), f32[64]{0:T(128)S(1)}, s32[]{:S(2)}) %slice-start.1) | async-done | bytes 280 | tf_op jit(solution)/shard_map/slice | solution.py:105
  26.7 0.1 select_add_fusion
  26.8 0.2 fusion.49
  27.0 0.2 fusion.50
  27.2 0.0 copy-start.2
  27.2 9.4 %all_gather.9 = f32[2,16,1024]{2,1,0:T(8,128)S(1)} all-gather(f32[2,16,128]{2,1,0:T(8,128)S(1)} %copy-done), channel_id=1, replica_groups=mesh['row'=8,'grp'=4] {'row'}, dimensions={2}, use_global_device_ids=true | all-gather | bytes 147456 | tf_op jit(solution)/shard_map/all_gather | solution.py:117
  36.7 0.0 copy-done.2
  36.7 9.2 %while.18 = (s32[]{:T(128)}, f32[16,128]{1,0:T(8,128)S(1)}, f32[16,128]{1,0:T(8,128)S(1)}, f32[128]{0:T(128)S(1)}, f32[2,16,1024]{2,1,0:T(8,128)S(1)}, /*index=5...) while((s32[]{:T(128)}, f32[16,128]{1,0:T(8,128)S(1)}, ...), condition=%wide.region_2.3_spmd.clone, body=%wide.region_0.2_spmd.clone.sunk | while | flops 54735752 | bytes 3901691 | solution.py:97
  36.7 0.1 dynamic_slice.69
  36.8 0.2 broadcast_subtract_fusion.3
  36.9 1.6 %fusion.83 = f32[128]{0:T(128)S(1)} fusion(f32[512,1]{0,1:T(1,128)S(1)} %bitcast.143, f32[128,512]{1,0:T(8,128)S(1)} %get-tuple-element.288, f32[3,128,512]{2,1,0:T(8,128)S(1)} %get-tuple-element.289, s32[512]{0:T(512)S(1)} %iota_add_fusion.4, s32[128]{0:T(128)S(1)} %iota_add_fusion.5, f32[128]{0:T(128)S(1)} %get-tuple-element.309, pred[]{:T(512)S(6)} %compare.3), kind=kOutput, calls=%fused_computation.6.clone.1 | convolution fusion | flops 2162944 | bytes 529921 | tf_op jit(solution)/shard_map/while/body/eval_jaxpr/dot_general | solution.py:94
  38.5 1.5 %fusion.82 = (f32[128,512]{1,0:T(8,128)S(1)}, f32[128,512]{1,0:T(8,128)S(1)}) fusion(f32[128,512]{1,0:T(8,128)S(1)} %get-tuple-element.288, f32[3,128,512]{2,1,0:T(8,128)S(1)} %get-tuple-element.289, s32[512]{0:T(512)S(1)} %iota_add_fusion.4, s32[128]{0:T(128)S(1)} %iota_add_fusion.5), kind=kLoop, calls=%fused_computation.20.clone.1 | loop fusion | flops 1703936 | bytes 1051136 | tf_op jit(solution)/shard_map/while/body/eval_jaxpr/jit(_where)/select_n | solution.py:26
  40.0 0.3 convolution_add_fusion.7
  40.2 0.3 convolution_subtract_fusion.3
  40.6 0.3 convolution_add_fusion.8
  40.9 0.3 convolution_add_fusion.9
  41.3 0.1 dynamic_slice.69
  41.4 0.2 broadcast_subtract_fusion.3
  41.5 1.6 %fusion.83 = f32[128]{0:T(128)S(1)} fusion(f32[512,1]{0,1:T(1,128)S(1)} %bitcast.143, f32[128,512]{1,0:T(8,128)S(1)} %get-tuple-element.288, f32[3,128,512]{2,1,0:T(8,128)S(1)} %get-tuple-element.289, s32[512]{0:T(512)S(1)} %iota_add_fusion.4, s32[128]{0:T(128)S(1)} %iota_add_fusion.5, f32[128]{0:T(128)S(1)} %get-tuple-element.309, pred[]{:T(512)S(6)} %compare.3), kind=kOutput, calls=%fused_computation.6.clone.1 | convolution fusion | flops 2162944 | bytes 529921 | tf_op jit(solution)/shard_map/while/body/eval_jaxpr/dot_general | solution.py:94
  43.1 1.5 %fusion.82 = (f32[128,512]{1,0:T(8,128)S(1)}, f32[128,512]{1,0:T(8,128)S(1)}) fusion(f32[128,512]{1,0:T(8,128)S(1)} %get-tuple-element.288, f32[3,128,512]{2,1,0:T(8,128)S(1)} %get-tuple-element.289, s32[512]{0:T(512)S(1)} %iota_add_fusion.4, s32[128]{0:T(128)S(1)} %iota_add_fusion.5), kind=kLoop, calls=%fused_computation.20.clone.1 | loop fusion | flops 1703936 | bytes 1051136 | tf_op jit(solution)/shard_map/while/body/eval_jaxpr/jit(_where)/select_n | solution.py:26
  44.6 0.3 convolution_add_fusion.7
  44.8 0.3 convolution_subtract_fusion.3
  45.2 0.3 convolution_add_fusion.8
  45.5 0.3 convolution_add_fusion.9
  45.9 0.2 fusion.44
  46.1 0.0 copy-start.3
  46.1 0.0 copy-start.4
  46.1 0.2 fusion.46
  46.3 0.5 %copy-done.3 = f32[2,16,128]{2,1,0:T(8,128)S(1)} copy-done((f32[2,16,128]{2,1,0:T(8,128)S(1)}, f32[2,16,128]{2,1,0:T(8,128)}, u32[]{:S(2)}) %copy-start.3) | copy-done | bytes 16408
  46.8 0.0 copy-done.4
  46.9 0.6 %multiply_add_fusion = (f32[2,16,128]{2,1,0:T(8,128)}, f32[2,16,128]{2,1,0:T(8,128)}) fusion(f32[2,16,128]{2,1,0:T(8,128)S(1)} %copy-done.3, f32[1,16,128]{2,1,0:T(8,128)S(1)} %fusion.44, f32[1,16,128]{2,1,0:T(8,128)S(1)} %fusion.46, f32[2,16,128]{2,1,0:T(8,128)S(1)} %copy-done.4), kind=kLoop, calls=%fused_computation.90 | loop fusion | flops 20480 | bytes 81920 | tf_op jit(solution)/shard_map/add | solution.py:138
  (12 shorter events, 0.1 us)
Async XLA Ops:
  0.6 0.8 %copy-start.1 = (f32[3,1024]{1,0:T(4,128)S(1)}, f32[3,1024]{1,0:T(4,128)}, u32[]{:S(2)}) copy-start(f32[3,1024]{1,0:T(4,128)} %param.8) | copy-start | bytes 36868
  0.6 0.7 %copy-start.5 = (f32[1024]{0:T(1024)S(1)}, f32[1024]{0:T(1024)}, u32[]{:S(2)}) copy-start(f32[1024]{0:T(1024)} %param.9) | copy-start | bytes 12292
  1.4 0.7 %copy-start.6 = (f32[128]{0:T(128)S(1)}, f32[128]{0:T(128)}, u32[]{:S(2)}) copy-start(f32[128]{0:T(128)} %param.10) | copy-start | bytes 1540
  1.4 11.0 %copy-start = (f32[2,16,128]{2,1,0:T(8,128)S(1)}, f32[2,16,128]{2,1,0:T(8,128)}, u32[]{:S(2)}) copy-start(f32[2,16,128]{2,1,0:T(8,128)} %param.12) | copy-start | bytes 49156
  12.4 13.4 %slice-start = ((f32[3,1024]{1,0:T(4,128)}), f32[3,64]{1,0:T(4,128)S(1)}, s32[]{:S(2)}) async-start(f32[3,1024]{1,0:T(4,128)} %param.8), calls=%async_computation | async-start | bytes 4096 | tf_op jit(solution)/shard_map/slice | solution.py:104
  26.0 0.7 %slice-start.1 = ((f32[1024]{0:T(1024)}), f32[64]{0:T(128)S(1)}, s32[]{:S(2)}) async-start(f32[1024]{0:T(1024)} %param.9), calls=%async_computation.1 | async-start | bytes 1024 | tf_op jit(solution)/shard_map/slice | solution.py:105
  27.2 9.4 %copy-start.2 = (f32[3,1024]{1,0:T(4,128)S(1)}, f32[3,1024]{1,0:T(4,128)}, u32[]{:S(2)}) copy-start(f32[3,1024]{1,0:T(4,128)} %param.8) | copy-start | bytes 36868
  46.1 0.7 %copy-start.3 = (f32[2,16,128]{2,1,0:T(8,128)S(1)}, f32[2,16,128]{2,1,0:T(8,128)}, u32[]{:S(2)}) copy-start(f32[2,16,128]{2,1,0:T(8,128)} %param.13) | copy-start | bytes 49156
  46.1 0.7 %copy-start.4 = (f32[2,16,128]{2,1,0:T(8,128)S(1)}, f32[2,16,128]{2,1,0:T(8,128)}, u32[]{:S(2)}) copy-start(f32[2,16,128]{2,1,0:T(8,128)} %param.11) | copy-start | bytes 49156
where the time goes:
time: 47.9 us; the launch traced here: 47.5 us
  blocking collectives  33 us (69%)
  matrix products  6.46 us (13%)
  other arithmetic  4.29 us (9%)
  local copies, waits for them, and re-layouts  2.78 us (6%)
  between operations  0.77 us (2%)
    all_gather x1, blocking collectives, local(): full_slab = lax.all_gather(section, 'grp', axis=1, tiled=True)  13.4 us
    all_gather x1, blocking collectives, local(): lax.all_gather(pop_piece, 'row', axis=2, tiled=True)  10.3 us
    all_gather x1, blocking collectives, local(): lax.all_gather(section, 'row', axis=2, tiled=True)  9.43 us
    dot_general x2, matrix products, one_block(): jnp.dot(h_real, pop_block, precision=lax.Precision.HIGHEST)  3.13 us
    select_n x2, other arithmetic, coupling(): return (jnp.where(on_diag, 0.0, h_real), jnp.where(on_diag, 0.0, h_imag))  2.93 us
    dot_general x8, matrix products, cross_rows(): lax.dot_general(slab_part, tile, (((1,), (1,)), ((), ())), precision=lax....  2.46 us
    unnamed x14, local copies, waits for them, and re-layouts  1.88 us

commit v1 on v0

--- a/solution.py
+++ b/solution.py
@@ -114,7 +114,7 @@
     z_real, z_imag, shift = accumulate(
         initial,
         (
-            lax.all_gather(section, "row", axis=2, tiled=True),
+            jnp.concatenate(lax.all_gather(section, "row"), axis=2),
             lax.all_gather(pop_piece, "row", axis=2, tiled=True),
         ),
         pos_rows,

time: 47.9 us -> 48.4 us (1.010)
  local copies, waits for them, and re-layouts: 2.78 us -> 3.48 us
    unnamed x14, local copies, waits for them, and re-layouts: 1.88 us -> 2.58 us
where the time goes in v1:
time: 48.4 us; the launch traced here: 48 us
  blocking collectives  32.8 us (68%)
  matrix products  6.46 us (13%)
  other arithmetic  4.29 us (9%)
  local copies, waits for them, and re-layouts  3.48 us (7%)
  between operations  0.77 us (2%)
    all_gather x1, blocking collectives, local(): full_slab = lax.all_gather(section, 'grp', axis=1, tiled=True)  13.4 us
    all_gather x1, blocking collectives, local(): lax.all_gather(pop_piece, 'row', axis=2, tiled=True)  10.3 us
    all_gather x1, blocking collectives, local(): lax.all_gather(section, 'row')  9.2 us
    dot_general x2, matrix products, one_block(): jnp.dot(h_real, pop_block, precision=lax.Precision.HIGHEST)  3.13 us
    select_n x2, other arithmetic, coupling(): return (jnp.where(on_diag, 0.0, h_real), jnp.where(on_diag, 0.0, h_imag))  2.93 us
    unnamed x14, local copies, waits for them, and re-layouts  2.58 us
    dot_general x8, matrix products, cross_rows(): lax.dot_general(slab_part, tile, (((1,), (1,)), ((), ())), precision=lax....  2.46 us

profile of v1, /device:TPU:0, one launch (start us, length us, event | category | flops | bytes accessed | tf_op | source)
XLA Modules:
  0.0 48.0 jit_solution(2809724232625520852)
XLA Ops:
  0.6 0.0 copy-start.1
  0.6 0.0 copy-start.5
  0.7 0.7 %copy-done.5 = f32[1024]{0:T(1024)S(1)} copy-done((f32[1024]{0:T(1024)S(1)}, f32[1024]{0:T(1024)}, u32[]{:S(2)}) %copy-start.5) | copy-done | bytes 4120
  1.3 0.1 dynamic_slice.34
  1.4 0.0 copy-done.1
  1.4 0.0 copy-start.6
  1.4 0.0 copy-start
  1.4 0.6 %copy-done.6 = f32[128]{0:T(128)S(1)} copy-done((f32[128]{0:T(128)S(1)}, f32[128]{0:T(128)}, u32[]{:S(2)}) %copy-start.6) | copy-done | bytes 536
  2.1 10.3 %all-gather.2 = f32[8,1,128]{2,1,0:T(1,128)S(1)} all-gather(f32[1,1,128]{2,1,0:T(1,128)S(1)} %bitcast.154), channel_id=3, replica_groups=mesh['row'=8,'grp'=4] {'row'}, dimensions={0}, use_global_device_ids=true | all-gather | bytes 4608 | tf_op jit(solution)/shard_map/all_gather | solution.py:118
  12.4 0.0 copy-done
  12.4 0.0 slice-start
  12.4 13.4 %all_gather.15 = f32[2,64,128]{2,1,0:T(8,128)S(1)} all-gather(f32[2,16,128]{2,1,0:T(8,128)S(1)} %copy-done), channel_id=1, replica_groups=mesh['row'=8,'grp'=4] {'grp'}, dimensions={1}, use_global_device_ids=true | all-gather | bytes 81920 | tf_op jit(solution)/shard_map/all_gather | solution.py:110
  25.7 0.0 slice-done
  25.8 0.1 broadcast_subtract_fusion.1
  25.9 0.2 fusion.52
  26.0 0.0 slice-start.1
  26.0 0.6 %slice-done.1 = f32[64]{0:T(128)S(1)} async-done(((f32[1024]{0:T(1024)}), f32[64]{0:T(128)S(1)}, s32[]{:S(2)}) %slice-start.1) | async-done | bytes 280 | tf_op jit(solution)/shard_map/slice | solution.py:105
  26.7 0.1 select_add_fusion
  26.8 0.2 fusion.49
  27.0 0.2 fusion.50
  27.2 9.2 %all-gather = f32[16,16,128]{2,1,0:T(8,128)S(1)} all-gather(f32[2,16,128]{2,1,0:T(8,128)S(1)} %copy-done), channel_id=2, replica_groups=mesh['row'=8,'grp'=4] {'row'}, dimensions={0}, use_global_device_ids=true | all-gather | bytes 147456 | tf_op jit(solution)/shard_map/all_gather | solution.py:117
  36.4 0.0 copy-start.2
  36.4 0.7 %copy-done.2 = f32[3,1024]{1,0:T(4,128)S(1)} copy-done((f32[3,1024]{1,0:T(4,128)S(1)}, f32[3,1024]{1,0:T(4,128)}, u32[]{:S(2)}) %copy-start.2) | copy-done | bytes 12312
  37.1 9.2 %while.18 = (s32[]{:T(128)}, f32[16,128]{1,0:T(8,128)S(1)}, f32[16,128]{1,0:T(8,128)S(1)}, f32[128]{0:T(128)S(1)}, f32[2,16,1024]{2,1,0:T(8,128)S(1)}, /*index=5...) while((s32[]{:T(128)}, f32[16,128]{1,0:T(8,128)S(1)}, ...), condition=%wide.region_2.3_spmd.clone, body=%wide.region_0.2_spmd.clone.sunk | while | flops 54735752 | bytes 3901691 | solution.py:97
  37.2 0.1 dynamic_slice.69
  37.2 0.2 broadcast_subtract_fusion.3
  37.4 1.6 %fusion.83 = f32[128]{0:T(128)S(1)} fusion(f32[512,1]{0,1:T(1,128)S(1)} %bitcast.152, f32[128,512]{1,0:T(8,128)S(1)} %get-tuple-element.288, f32[3,128,512]{2,1,0:T(8,128)S(1)} %get-tuple-element.289, s32[512]{0:T(512)S(1)} %iota_add_fusion.4, s32[128]{0:T(128)S(1)} %iota_add_fusion.5, f32[128]{0:T(128)S(1)} %get-tuple-element.309, pred[]{:T(512)S(6)} %compare.3), kind=kOutput, calls=%fused_computation.6.clone.1 | convolution fusion | flops 2162944 | bytes 529921 | tf_op jit(solution)/shard_map/while/body/eval_jaxpr/dot_general | solution.py:94
  39.0 1.5 %fusion.82 = (f32[128,512]{1,0:T(8,128)S(1)}, f32[128,512]{1,0:T(8,128)S(1)}) fusion(f32[128,512]{1,0:T(8,128)S(1)} %get-tuple-element.288, f32[3,128,512]{2,1,0:T(8,128)S(1)} %get-tuple-element.289, s32[512]{0:T(512)S(1)} %iota_add_fusion.4, s32[128]{0:T(128)S(1)} %iota_add_fusion.5), kind=kLoop, calls=%fused_computation.20.clone.1 | loop fusion | flops 1703936 | bytes 1051136 | tf_op jit(solution)/shard_map/while/body/eval_jaxpr/jit(_where)/select_n | solution.py:26
  40.4 0.3 convolution_add_fusion.7
  40.7 0.3 convolution_subtract_fusion.3
  41.0 0.3 convolution_add_fusion.8
  41.4 0.3 convolution_add_fusion.9
  41.8 0.1 dynamic_slice.69
  41.9 0.2 broadcast_subtract_fusion.3
  42.0 1.6 %fusion.83 = f32[128]{0:T(128)S(1)} fusion(f32[512,1]{0,1:T(1,128)S(1)} %bitcast.152, f32[128,512]{1,0:T(8,128)S(1)} %get-tuple-element.288, f32[3,128,512]{2,1,0:T(8,128)S(1)} %get-tuple-element.289, s32[512]{0:T(512)S(1)} %iota_add_fusion.4, s32[128]{0:T(128)S(1)} %iota_add_fusion.5, f32[128]{0:T(128)S(1)} %get-tuple-element.309, pred[]{:T(512)S(6)} %compare.3), kind=kOutput, calls=%fused_computation.6.clone.1 | convolution fusion | flops 2162944 | bytes 529921 | tf_op jit(solution)/shard_map/while/body/eval_jaxpr/dot_general | solution.py:94
  43.6 1.5 %fusion.82 = (f32[128,512]{1,0:T(8,128)S(1)}, f32[128,512]{1,0:T(8,128)S(1)}) fusion(f32[128,512]{1,0:T(8,128)S(1)} %get-tuple-element.288, f32[3,128,512]{2,1,0:T(8,128)S(1)} %get-tuple-element.289, s32[512]{0:T(512)S(1)} %iota_add_fusion.4, s32[128]{0:T(128)S(1)} %iota_add_fusion.5), kind=kLoop, calls=%fused_computation.20.clone.1 | loop fusion | flops 1703936 | bytes 1051136 | tf_op jit(solution)/shard_map/while/body/eval_jaxpr/jit(_where)/select_n | solution.py:26
  45.1 0.3 convolution_add_fusion.7
  45.3 0.3 convolution_subtract_fusion.3
  45.7 0.3 convolution_add_fusion.8
  46.0 0.3 convolution_add_fusion.9
  46.3 0.2 fusion.44
  46.6 0.0 copy-start.3
  46.6 0.0 copy-start.4
  46.6 0.2 fusion.46
  46.8 0.5 %copy-done.3 = f32[2,16,128]{2,1,0:T(8,128)S(1)} copy-done((f32[2,16,128]{2,1,0:T(8,128)S(1)}, f32[2,16,128]{2,1,0:T(8,128)}, u32[]{:S(2)}) %copy-start.3) | copy-done | bytes 16408
  47.3 0.0 copy-done.4
  47.3 0.6 %multiply_add_fusion = (f32[2,16,128]{2,1,0:T(8,128)}, f32[2,16,128]{2,1,0:T(8,128)}) fusion(f32[2,16,128]{2,1,0:T(8,128)S(1)} %copy-done.3, f32[1,16,128]{2,1,0:T(8,128)S(1)} %fusion.44, f32[1,16,128]{2,1,0:T(8,128)S(1)} %fusion.46, f32[2,16,128]{2,1,0:T(8,128)S(1)} %copy-done.4), kind=kLoop, calls=%fused_computation.91 | loop fusion | flops 20480 | bytes 81920 | tf_op jit(solution)/shard_map/add | solution.py:138
  (13 shorter events, 0.1 us)
Async XLA Ops:
  0.6 0.8 %copy-start.1 = (f32[3,1024]{1,0:T(4,128)S(1)}, f32[3,1024]{1,0:T(4,128)}, u32[]{:S(2)}) copy-start(f32[3,1024]{1,0:T(4,128)} %param.8) | copy-start | bytes 36868
  0.6 0.7 %copy-start.5 = (f32[1024]{0:T(1024)S(1)}, f32[1024]{0:T(1024)}, u32[]{:S(2)}) copy-start(f32[1024]{0:T(1024)} %param.9) | copy-start | bytes 12292
  1.4 0.7 %copy-start.6 = (f32[128]{0:T(128)S(1)}, f32[128]{0:T(128)}, u32[]{:S(2)}) copy-start(f32[128]{0:T(128)} %param.10) | copy-start | bytes 1540
  1.4 11.0 %copy-start = (f32[2,16,128]{2,1,0:T(8,128)S(1)}, f32[2,16,128]{2,1,0:T(8,128)}, u32[]{:S(2)}) copy-start(f32[2,16,128]{2,1,0:T(8,128)} %param.12) | copy-start | bytes 49156
  12.4 13.4 %slice-start = ((f32[3,1024]{1,0:T(4,128)}), f32[3,64]{1,0:T(4,128)S(1)}, s32[]{:S(2)}) async-start(f32[3,1024]{1,0:T(4,128)} %param.8), calls=%async_computation | async-start | bytes 4096 | tf_op jit(solution)/shard_map/slice | solution.py:104
  26.0 0.7 %slice-start.1 = ((f32[1024]{0:T(1024)}), f32[64]{0:T(128)S(1)}, s32[]{:S(2)}) async-start(f32[1024]{0:T(1024)} %param.9), calls=%async_computation.1 | async-start | bytes 1024 | tf_op jit(solution)/shard_map/slice | solution.py:105
  36.4 0.7 %copy-start.2 = (f32[3,1024]{1,0:T(4,128)S(1)}, f32[3,1024]{1,0:T(4,128)}, u32[]{:S(2)}) copy-start(f32[3,1024]{1,0:T(4,128)} %param.8) | copy-start | bytes 36868
  46.6 0.7 %copy-start.3 = (f32[2,16,128]{2,1,0:T(8,128)S(1)}, f32[2,16,128]{2,1,0:T(8,128)}, u32[]{:S(2)}) copy-start(f32[2,16,128]{2,1,0:T(8,128)} %param.13) | copy-start | bytes 49156
  46.6 0.7 %copy-start.4 = (f32[2,16,128]{2,1,0:T(8,128)S(1)}, f32[2,16,128]{2,1,0:T(8,128)}, u32[]{:S(2)}) copy-start(f32[2,16,128]{2,1,0:T(8,128)} %param.11) | copy-start | bytes 49156
